TPU v7x, 32 devices: a whole 2x2x4 slice. The times are simulated.
32 devices in a mesh: cp: 16 (over z, x, core), tp: 2 (over y).
Axes of the slice: x: 2, y: 2, z: 4, core: 2. Of those that a mesh axis runs over, the one named last changes fastest.
Arguments:
- hidden: bfloat16 [8192, 4096], P('cp', 'tp'), may hold values from -6 to 6
- norm_gain: float32 [4096], replicated, may hold values from 0.5 to 1.5
- w_query: bfloat16 [4096, 4096], P(None, 'tp'), may hold values from -0.140625 to 0.140625
- w_key: bfloat16 [4096, 1024], P(None, 'tp'), may hold values from -4 to 4
- w_value: bfloat16 [4096, 1024], P(None, 'tp'), may hold values from -0.09375 to 0.09375
- w_out: bfloat16 [4096, 4096], P('tp'), may hold values from -0.5 to 0.5
- doc_ids: int32 [8192], P('cp'), may hold values from 0 to 5, never falling along the last dimension, each value on 1 to 6144 neighbouring positions
Outputs:
- updated: bfloat16 [8192, 4096], P('cp', 'tp')
Inputs may be any that keep to these rules, and one draw needn't show every extreme that they name: `doc_ids`: document numbers never fall along the sequence; every document has 1 to 6144 tokens.
All inputs are finite; a program needn't handle non-finite values.
Results may differ from a plain program's by a relative error of at most 0.017.
The roundings to bfloat16 on the way count: a program that leaves them out, or rounds other values in their place, can miss the bound.
Values may be sent and summed in bfloat16 or wider, within the bound.
A program may use at most 128 MiB of HBM per device.

v0:
```python
import jax
import jax.numpy as jnp
from jax import lax
from jax.sharding import PartitionSpec as P

HEADS = 32
KV_HEADS = 8
HEAD_SIZE = 128
epsilon = 1e-05
rope_base = 500000.0


def rotate(vectors, positions):
    half = HEAD_SIZE // 2
    freqs = rope_base ** (-jnp.arange(half, dtype=jnp.float32) * 2.0 / HEAD_SIZE)
    angles = positions.astype(jnp.float32)[:, None] * freqs[None, :]
    cosine = jnp.cos(angles)[:, None, :]
    sine = jnp.sin(angles)[:, None, :]
    first = vectors[..., :half]
    second = vectors[..., half:]
    return jnp.concatenate(
        [first * cosine - second * sine, second * cosine + first * sine], axis=-1
    )


def attend_block(
    loop_state, query_matrix, query_pos, query_doc, key_matrix, value_matrix, key_pos, key_doc
):
    best, total, running_output = loop_state
    logit_matrix = jnp.einsum(
        "ucpm,ycm->cpuy", query_matrix, key_matrix, preferred_element_type=jnp.float32
    ) * HEAD_SIZE ** (-0.5)
    allowed = (key_pos[None, :] <= query_pos[:, None]) & (key_doc[None, :] == query_doc[:, None])
    masked = jnp.where(allowed, logit_matrix, jnp.float32(-1e30))
    new_best = jnp.maximum(best, jnp.max(masked, axis=-1))
    correction_scale = jnp.exp(best - new_best)
    attention_weights = jnp.where(
        allowed, jnp.exp(logit_matrix - new_best[..., None]), jnp.float32(0.0)
    )
    total = total * correction_scale + jnp.sum(attention_weights, axis=-1)
    running_output = running_output * correction_scale[..., None] + jnp.einsum(
        "sfec,csh->sfeh",
        attention_weights.astype(jnp.bfloat16),
        value_matrix,
        preferred_element_type=jnp.float32,
    )
    return (new_best, total, running_output)


def shards(hidden, norm_gain, w_query, w_key, w_value, w_out, doc_ids):
    tok_rows = hidden.shape[0]
    half_rows = tok_rows // 2
    width = norm_gain.shape[0]
    group = HEADS // KV_HEADS
    local_kv = w_key.shape[1] // HEAD_SIZE
    query_cols = w_query.shape[1]
    key_cols = w_key.shape[1]
    wide_local = hidden.astype(jnp.float32)
    squares = lax.psum(jnp.sum(wide_local * wide_local, axis=1), "tp")
    inverse_rms = lax.rsqrt(squares / width + epsilon)[:, None]
    piece = lax.all_gather(hidden, "tp", axis=1, tiled=True)
    normed_piece = (piece.astype(jnp.float32) * inverse_rms * norm_gain[None, :]).astype(
        jnp.bfloat16
    )
    projected = jnp.concatenate(
        [
            jnp.dot(normed_piece, w_query, preferred_element_type=jnp.float32),
            jnp.dot(normed_piece, w_key, preferred_element_type=jnp.float32),
            jnp.dot(normed_piece, w_value, preferred_element_type=jnp.float32),
        ],
        axis=1,
    )
    cp_rank = lax.axis_index("cp")
    positions = cp_rank * tok_rows + jnp.arange(tok_rows, dtype=jnp.int32)
    query_raw = projected[:, :query_cols].reshape(tok_rows, local_kv * group, HEAD_SIZE)
    key_raw = projected[:, query_cols : query_cols + key_cols].reshape(
        tok_rows, local_kv, HEAD_SIZE
    )
    query_matrix = (
        rotate(query_raw, positions)
        .astype(jnp.bfloat16)
        .reshape(tok_rows, local_kv, group, HEAD_SIZE)
    )
    keys_flat = rotate(key_raw, positions).astype(jnp.bfloat16).reshape(tok_rows, key_cols)
    values_flat = projected[:, query_cols + key_cols :].astype(jnp.bfloat16)
    query_doc = doc_ids.astype(jnp.float32)
    docs_flat = query_doc.astype(jnp.bfloat16)
    first_queries = query_matrix[:half_rows]
    first_pos = positions[:half_rows]
    first_doc = query_doc[:half_rows]
    second_queries = query_matrix[half_rows:]
    second_doc = query_doc[half_rows:]
    second_start = cp_rank * tok_rows + half_rows
    second_pos = second_start + jnp.arange(half_rows, dtype=jnp.int32)
    last_first = cp_rank * tok_rows + half_rows - 1
    last_second = second_start + half_rows - 1
    init_half = (
        jnp.full((local_kv, group, half_rows), -1e30, jnp.float32),
        jnp.zeros((local_kv, group, half_rows), jnp.float32),
        jnp.zeros((local_kv, group, half_rows, HEAD_SIZE), jnp.float32),
    )
    init = (init_half, init_half)
    key_piece = lax.all_gather(keys_flat, "cp", axis=0, tiled=True)
    value_piece = lax.all_gather(values_flat, "cp", axis=0, tiled=True)
    doc_piece = lax.all_gather(docs_flat, "cp", axis=0, tiled=True)
    count = key_piece.shape[0]

    def inner(index, state):
        first_state, second_state = state
        offset = index * tok_rows
        key_blk = lax.dynamic_slice_in_dim(key_piece, offset, tok_rows, 0).reshape(
            tok_rows, local_kv, HEAD_SIZE
        )
        value_blk = lax.dynamic_slice_in_dim(value_piece, offset, tok_rows, 0).reshape(
            tok_rows, local_kv, HEAD_SIZE
        )
        key_doc = lax.dynamic_slice_in_dim(doc_piece, offset, tok_rows, 0).astype(jnp.float32)
        key_pos = offset + jnp.arange(tok_rows, dtype=jnp.int32)

        def attend_first(inner_state):
            return attend_block(
                inner_state,
                first_queries,
                first_pos,
                first_doc,
                key_blk,
                value_blk,
                key_pos,
                key_doc,
            )

        def attend_second(inner_state):
            return attend_block(
                inner_state,
                second_queries,
                second_pos,
                second_doc,
                key_blk,
                value_blk,
                key_pos,
                key_doc,
            )

        first_state = lax.cond(
            offset <= last_first, attend_first, lambda inner_state: inner_state, first_state
        )
        second_state = lax.cond(
            offset <= last_second, attend_second, lambda inner_state: inner_state, second_state
        )
        return (first_state, second_state)

    final = lax.fori_loop(0, count // tok_rows, inner, init)

    def finish(state):
        result = state[2] / state[1][..., None]
        return (
            jnp.transpose(result, (2, 0, 1, 3)).reshape(half_rows, query_cols).astype(jnp.bfloat16)
        )

    attended_first = finish(final[0])
    attended_second = finish(final[1])
    attended = jnp.concatenate([attended_first, attended_second], axis=0)
    terms = jnp.dot(attended, w_out, preferred_element_type=jnp.float32)
    summed = lax.psum_scatter(terms.astype(jnp.bfloat16), "tp", scatter_dimension=1, tiled=True)
    return summed


def solution(mesh):
    in_specs = (
        P("cp", "tp"),
        P(),
        P(None, "tp"),
        P(None, "tp"),
        P(None, "tp"),
        P("tp", None),
        P("cp"),
    )
    out_specs = P("cp", "tp")
    return jax.shard_map(shards, mesh=mesh, in_specs=in_specs, out_specs=out_specs, check_vma=False)
```

profile of v0, /device:TPU:0, one launch (start us, length us, event | category | flops | bytes accessed | tf_op | source)
XLA Modules:
  0.0 622.3 jit_solution(9094426565222155319)
XLA Ops:
  7.3 2.1 multiply_reduce_fusion
  9.4 5.9 psum.7
  15.8 52.5 %all-gather.5.cloned.1.call-done = bf16[512,4096]{1,0:T(8,128)(2,1)} async-done(((bf16[512,2048]{1,0:T(8,128)(2,1)}), bf16[512,4096]{1,0:T(8,128)(2,1)}) %all-gather.5.cloned.1.call-update) | async-done | bytes 4194320 | tf_op jit(solution)/shard_map/all_gather | solution.py:61
  68.4 5.9 fusion.44
  75.4 6.6 %convolution_convert_fusion.1 = bf16[512,512]{1,0:T(8,128)(2,1)} fusion(bf16[4096,512]{1,0:T(8,128)(2,1)} %param.17, bf16[512,4096]{1,0:T(8,128)(2,1)} %all-gather.5.cloned.1.call-done, f32[4096]{0:T(1024)S(1)} %copy-done.7, f32[512]{0:T(512)S(1)} %add_rsqrt_fusion), kind=kOutput, calls=%fused_computation.61 | convolution fusion | flops 2156134400 | bytes 8931328 | tf_op jit(solution)/shard_map/dot_general | solution.py:69
  82.4 22.4 %all-gather = bf16[16,1,512]{2,1,0:T(2,128)(2,1)S(1)} all-gather(bf16[1,1,512]{2,1,0:T(2,128)(2,1)S(1)} %reshape.106), channel_id=1, replica_groups=mesh['cp'=16,'tp'=2] {'cp'}, dimensions={0}, use_global_device_ids=true | all-gather | bytes 17408 | tf_op jit(solution)/shard_map/all_gather | solution.py:105
  105.0 13.1 %convolution_bitcast_fusion = f32[64,8,16,128]{3,1,2,0:T(8,128)S(1)} fusion(bf16[4096,2048]{1,0:T(8,128)(2,1)} %param.15, bf16[512,4096]{1,0:T(8,128)(2,1)} %all-gather.5.cloned.1.call-done, f32[4096]{0:T(1024)S(1)} %copy-done.7, f32[512]{0:T(512)S(1)} %add_rsqrt_fusion), kind=kOutput, calls=%fused_computation.53 | convolution fusion | flops 8598323200 | bytes 25184256 | tf_op jit(solution)/shard_map/dot_general | solution.py:67
  119.0 1.6 add_convert_fusion
  120.6 1.2 pad_maximum_fusion
  122.3 31.2 %all-gather.7.cloned.1.call-done = bf16[8192,512]{0,1:T(8,128)(2,1)} async-done(((bf16[512,512]{0,1:T(8,128)(2,1)}), bf16[8192,512]{0,1:T(8,128)(2,1)}) %all-gather.7.cloned.1.call-update) | async-done | bytes 8388624 | tf_op jit(solution)/shard_map/all_gather | solution.py:103
  153.5 74.7 %all-gather.9.cloned.1.call-done = bf16[8192,512]{1,0:T(8,128)(2,1)} async-done(((bf16[512,512]{1,0:T(8,128)(2,1)}), bf16[8192,512]{1,0:T(8,128)(2,1)}) %all-gather.9.cloned.1.call-update) | async-done | bytes 8388624 | tf_op jit(solution)/shard_map/all_gather | solution.py:104
  228.2 1.5 broadcast_in_dim.42
  229.7 1.6 broadcast_in_dim.42.clone
  231.3 68.3 %while.24 = (s32[]{:T(128)}, f32[4,4,256]{2,1,0:T(4,128)S(1)}, f32[4,4,256]{2,1,0:T(4,128)S(1)}, f32[4,4,256,128]{3,2,1,0:T(8,128)}, f32[4,4,256]{2,1,0:T(4,128)...) while((s32[]{:T(128)}, f32[4,4,256]{2,1,0:T(4,128)S(1)}, ...), condition=%wide.region_11.12_spmd.clone, body=%wide.region_2.11_spmd.clone.sunk | while | flops 2196522240 | bytes 105403112 | solution.py:152
  232.4 1.1 constant_dynamic-slice_fusion.5
  234.5 8.1 %conditional.6 = ((f32[4,4,256]{2,1,0:T(4,128)S(1)}, f32[4,4,256]{2,1,0:T(4,128)S(1)}, f32[4,4,256,128]{3,2,1,0:T(8,128)})) conditional(s32[]{:T(128)} %convert_element_type.128, (f32[4,4,256]{2,1,0:T(4,128)S(1)}, f32[4,4,256]{2,1,0:T(4,128)S(1)}, f32[4,4,256,128]{3,2,1,0:T(8,128)}) %tuple.72, (s32[512]{0:T(512)S(1)}, s32[256]{0:T(256)S(1)}, ...), branch_computations={%region_3.0_spmd, %region_4.6_spmd} | conditional | flops 1098260480 | bytes 51124340 | solution.py:144
  234.7 1.6 fusion.2
  236.3 1.7 fusion.6
  238.1 3.2 multiply_add_fusion
  241.3 1.3 copy-done.3
  242.6 8.1 %conditional.7 = ((f32[4,4,256]{2,1,0:T(4,128)S(1)}, f32[4,4,256]{2,1,0:T(4,128)S(1)}, f32[4,4,256,128]{3,2,1,0:T(8,128)})) conditional(s32[]{:T(128)} %convert_element_type.129, (f32[4,4,256]{2,1,0:T(4,128)S(1)}, f32[4,4,256]{2,1,0:T(4,128)S(1)}, f32[4,4,256,128]{3,2,1,0:T(8,128)}) %tuple.74, (s32[512]{0:T(512)S(1)}, s32[]{:T(128)}, ...), branch_computations={%region_7.7_spmd, %region_8.10_spmd} | conditional | flops 1098260736 | bytes 51126392 | solution.py:147
  242.8 1.6 fusion.20
  244.4 1.7 fusion.24
  246.1 3.2 multiply_add_fusion.2
  249.3 1.3 copy-done.5
  251.8 1.1 constant_dynamic-slice_fusion.5
  255.1 1.1 constant_dynamic-slice_fusion.5
  299.6 1.9 copy.40
  301.5 2.9 copy.39
  304.4 2.1 divide_convert_fusion
  306.5 14.0 %convolution_convert_fusion = bf16[512,4096]{1,0:T(8,128)(2,1)} fusion(bf16[2048,4096]{1,0:T(8,128)(2,1)} %param.18, bf16[256,2048]{0,1:T(8,128)(2,1)S(1)} %bitcast.110, bf16[256,2048]{0,1:T(8,128)(2,1)S(1)} %bitcast.111), kind=kOutput, calls=%fused_computation.49 | convolution fusion | flops 8596226048 | bytes 23068672 | tf_op jit(solution)/shard_map/dot_general | solution.py:163
  320.5 295.2 %reduce-scatter.2.cloned.1.call-done = bf16[512,2048]{1,0:T(8,128)(2,1)} async-done(((bf16[512,4096]{1,0:T(8,128)(2,1)}), bf16[512,2048]{1,0:T(8,128)(2,1)}) %reduce-scatter.2.cloned.1.call-update) | async-done | bytes 2097168 | tf_op jit(solution)/shard_map/reduce_scatter | solution.py:164
  (176 shorter events, 53.6 us)
Async XLA Ops:
  6.5 61.8 %copy-start.7 = (f32[4096]{0:T(1024)S(1)}, f32[4096]{0:T(1024)}, u32[]{:S(2)}) copy-start(f32[4096]{0:T(1024)} %param.14) | copy-start | bytes 49156
  6.5 61.8 %all-gather.5.cloned.1.call-start = ((), (), s32[]{:S(2)}) async-start(), calls=%async_computation.1 | async-start | bytes 6291456 | tf_op jit(solution)/shard_map/all_gather | solution.py:61
  7.3 146.2 %all-gather.7.cloned.1.call-start = ((), (), s32[]{:S(2)}) async-start(), calls=%async_computation.2 | async-start | bytes 8912896 | tf_op jit(solution)/shard_map/all_gather | solution.py:103
  75.3 7.0 %copy-start.6 = (s32[512]{0:T(512)S(1)}, s32[512]{0:T(512)}, u32[]{:S(2)}) copy-start(s32[512]{0:T(512)} %param.19) | copy-start | bytes 6148
  75.4 152.8 %all-gather.9.cloned.1.call-start = ((), (), s32[]{:S(2)}) async-start(), calls=%async_computation.3 | async-start | bytes 8912896 | tf_op jit(solution)/shard_map/all_gather | solution.py:104
  82.1 533.7 %reduce-scatter.2.cloned.1.call-start = ((), (), s32[]{:S(2)}) async-start(), calls=%async_computation.4 | async-start | bytes 6291456 | tf_op jit(solution)/shard_map/reduce_scatter | solution.py:164
  236.3 1.8 copy-start
  236.3 1.8 copy-start.2
  241.2 1.3 copy-start.3
  244.4 1.8 copy-start.1
  244.4 1.8 copy-start.4
  249.3 1.3 copy-start.5
Sparse Core Ops, SparseCore 0:
  8.9 59.4 all-gather.4
  75.5 77.9 all-gather.6
  155.6 72.4 all-gather.8
  320.7 295.0 reduce-scatter.1
where the time goes:
time: 625 us; the launch traced here: 622 us
  waiting for transfers between devices  454 us (73%)
  local copies, waits for them, and re-layouts  63.1 us (10%)
  matrix products  49.1 us (8%)
  blocking collectives  28.3 us (5%)
  other arithmetic  13.6 us (2%)
  between operations  13.3 us (2%)
    reduce_scatter x1, waiting for transfers between devices, shards(): lax.psum_scatter(terms.astype(jnp.bfloat16), 'tp', scatter_dimension=1, t...  295 us
    all_gather x1, waiting for transfers between devices, shards(): value_piece = lax.all_gather(values_flat, 'cp', axis=0, tiled=True)  74.7 us
    all_gather x1, waiting for transfers between devices, shards(): piece = lax.all_gather(hidden, 'tp', axis=1, tiled=True)  52.5 us
    dynamic_slice x32, local copies, waits for them, and re-layouts, inner(): lax.dynamic_slice_in_dim(value_piece, offset, tok_rows, 0)  33.5 us
    all_gather x1, waiting for transfers between devices, shards(): key_piece = lax.all_gather(keys_flat, 'cp', axis=0, tiled=True)  31.2 us
    all_gather x1, blocking collectives, shards(): doc_piece = lax.all_gather(docs_flat, 'cp', axis=0, tiled=True)  22.4 us
    dynamic_slice x16, local copies, waits for them, and re-layouts, inner(): lax.dynamic_slice_in_dim(key_piece, offset, tok_rows, 0)  17.2 us
    dot_general x1, matrix products, shards(): terms = jnp.dot(attended, w_out, preferred_element_type=jnp.float32)  14 us
  transfers between devices with their start and end apart: 4, of which 4 were waited for; matrix products, arithmetic and copies ran while one was open for 4% of the time, Pallas kernels for 0%

commit v1 on v0

--- a/solution.py
+++ b/solution.py
@@ -101,7 +101,17 @@
     )
     init = (init_half, init_half)
     key_piece = lax.all_gather(keys_flat, "cp", axis=0, tiled=True)
-    value_piece = lax.all_gather(values_flat, "cp", axis=0, tiled=True)
+    length, mine, span = (lax.axis_size("cp"), lax.axis_index("cp"), values_flat.shape[0])
+    right = [(i, (i + 1) % length) for i in range(length)]
+    value_piece = jnp.zeros(
+        (*values_flat.shape[:0], length * span, *values_flat.shape[0 + 1 :]), values_flat.dtype
+    )
+    current = values_flat
+    for step in range(length):
+        source = (mine - step) % length
+        value_piece = lax.dynamic_update_slice_in_dim(value_piece, current, source * span, axis=0)
+        if step < length - 1:
+            current = lax.ppermute(current, "cp", right)
     doc_piece = lax.all_gather(docs_flat, "cp", axis=0, tiled=True)
     count = key_piece.shape[0]
 

time: 625 us -> 680 us (1.088)
  waiting for transfers between devices: 454 us -> 496 us
  local copies, waits for them, and re-layouts: 63.1 us -> 70 us
    ppermute x0 -> x15, waiting for transfers between devices: none -> 148 us  [shards(): current = lax.ppermute(current, 'cp', right)]
    all_gather x1 -> x0, waiting for transfers between devices: 74.7 us -> none  [shards(): value_piece = lax.all_gather(values_flat, 'cp', axis=0, tiled=True)]
    all_gather x1, waiting for transfers between devices: 31.2 us -> 0.01 us  [shards(): key_piece = lax.all_gather(keys_flat, 'cp', axis=0, tiled=True)]
    dynamic_slice x16 -> x0, local copies, waits for them, and re-layouts: 17.2 us -> none  [inner(): lax.dynamic_slice_in_dim(key_piece, offset, tok_rows, 0)]
    ppermute x0 -> x15, local copies, waits for them, and re-layouts: none -> 16.7 us  [shards(): current = lax.ppermute(current, 'cp', right)]
    dynamic_update_slice x0 -> x16, local copies, waits for them, and re-layouts: none -> 13.2 us  [shards(): lax.dynamic_update_slice_in_dim(value_piece, current, source * span, axis=0)]
    dynamic_slice x32 -> x16, local copies, waits for them, and re-layouts: 33.5 us -> 20.4 us  [inner(): lax.dynamic_slice_in_dim(value_piece, offset, tok_rows, 0)]
  transfers between devices with their start and end apart: 4 -> 18, of which waited for: 4 -> 14; matrix products, arithmetic and copies ran while one was open for 4% -> 9% of each run, Pallas kernels for 0% -> 0%
where the time goes in v1:
time: 680 us; the launch traced here: 673 us
  waiting for transfers between devices  496 us (73%)
  local copies, waits for them, and re-layouts  70 us (10%)
  matrix products  50.4 us (7%)
  blocking collectives  26.7 us (4%)
  between operations  14.1 us (2%)
  other arithmetic  13.7 us (2%)
    reduce_scatter x1, waiting for transfers between devices, shards(): lax.psum_scatter(terms.astype(jnp.bfloat16), 'tp', scatter_dimension=1, t...  295 us
    ppermute x15, waiting for transfers between devices, shards(): current = lax.ppermute(current, 'cp', right)  148 us
    all_gather x1, waiting for transfers between devices, shards(): piece = lax.all_gather(hidden, 'tp', axis=1, tiled=True)  52.5 us
    all_gather x1, blocking collectives, shards(): doc_piece = lax.all_gather(docs_flat, 'cp', axis=0, tiled=True)  20.8 us
    dynamic_slice x16, local copies, waits for them, and re-layouts, inner(): lax.dynamic_slice_in_dim(value_piece, offset, tok_rows, 0)  20.4 us
    ppermute x15, local copies, waits for them, and re-layouts, shards(): current = lax.ppermute(current, 'cp', right)  16.7 us
    dot_general x1, matrix products, shards(): jnp.dot(normed_piece, w_query, preferred_element_type=jnp.float32)  15.1 us
    dot_general x1, matrix products, shards(): terms = jnp.dot(attended, w_out, preferred_element_type=jnp.float32)  14.1 us
  transfers between devices with their start and end apart: 18, of which 14 were waited for; matrix products, arithmetic and copies ran while one was open for 9% of the time, Pallas kernels for 0%

profile of v1, /device:TPU:0, one launch (start us, length us, event | category | flops | bytes accessed | tf_op | source)
XLA Modules:
  0.0 672.9 jit_solution(5743082728802257074)
XLA Ops:
  7.3 2.1 multiply_reduce_fusion
  9.4 5.9 psum.7
  15.9 52.5 %all-gather.4.cloned.1.call-done = bf16[512,4096]{1,0:T(8,128)(2,1)} async-done(((bf16[512,2048]{1,0:T(8,128)(2,1)}), bf16[512,4096]{1,0:T(8,128)(2,1)}) %all-gather.4.cloned.1.call-update) | async-done | bytes 4194320 | tf_op jit(solution)/shard_map/all_gather | solution.py:61
  68.4 5.9 fusion.44
  75.4 5.8 convolution_convert_fusion.1
  81.3 17.0 %collective-permute-done = bf16[512,512]{1,0:T(8,128)(2,1)S(1)} collective-permute-done((bf16[512,512]{1,0:T(8,128)(2,1)S(1)}, bf16[512,512]{1,0:T(8,128)(2,1)S(1)}, u32[]{:S(2)}, u32[]{:S(2)}) %collective-permute-start) | collective-permute-done | bytes 524320 | tf_op jit(solution)/shard_map/ppermute | solution.py:114
  98.3 17.7 %collective-permute-done.1 = bf16[512,512]{1,0:T(8,128)(2,1)S(1)} collective-permute-done((bf16[512,512]{1,0:T(8,128)(2,1)S(1)}, bf16[512,512]{1,0:T(8,128)(2,1)S(1)}, u32[]{:S(2)}, u32[]{:S(2)}) %collective-permute-start.1) | collective-permute-done | bytes 524320 | tf_op jit(solution)/shard_map/ppermute | solution.py:114
  116.0 20.4 %collective-permute-done.2 = bf16[512,512]{1,0:T(8,128)(2,1)S(1)} collective-permute-done((bf16[512,512]{1,0:T(8,128)(2,1)S(1)}, bf16[512,512]{1,0:T(8,128)(2,1)S(1)}, u32[]{:S(2)}, u32[]{:S(2)}) %collective-permute-start.2) | collective-permute-done | bytes 524320 | tf_op jit(solution)/shard_map/ppermute | solution.py:114
  136.5 22.2 %collective-permute-done.3 = bf16[512,512]{1,0:T(8,128)(2,1)S(1)} collective-permute-done((bf16[512,512]{1,0:T(8,128)(2,1)S(1)}, bf16[512,512]{1,0:T(8,128)(2,1)S(1)}, u32[]{:S(2)}, u32[]{:S(2)}) %collective-permute-start.3) | collective-permute-done | bytes 524320 | tf_op jit(solution)/shard_map/ppermute | solution.py:114
  158.6 13.7 %collective-permute-done.4 = bf16[512,512]{1,0:T(8,128)(2,1)S(1)} collective-permute-done((bf16[512,512]{1,0:T(8,128)(2,1)S(1)}, bf16[512,512]{1,0:T(8,128)(2,1)S(1)}, u32[]{:S(2)}, u32[]{:S(2)}) %collective-permute-start.4) | collective-permute-done | bytes 524320 | tf_op jit(solution)/shard_map/ppermute | solution.py:114
  173.2 10.5 %collective-permute-done.5 = bf16[512,512]{1,0:T(8,128)(2,1)S(1)} collective-permute-done((bf16[512,512]{1,0:T(8,128)(2,1)S(1)}, bf16[512,512]{1,0:T(8,128)(2,1)S(1)}, u32[]{:S(2)}, u32[]{:S(2)}) %collective-permute-start.5) | collective-permute-done | bytes 524320 | tf_op jit(solution)/shard_map/ppermute | solution.py:114
  183.7 11.3 %collective-permute-done.6 = bf16[512,512]{1,0:T(8,128)(2,1)S(1)} collective-permute-done((bf16[512,512]{1,0:T(8,128)(2,1)S(1)}, bf16[512,512]{1,0:T(8,128)(2,1)S(1)}, u32[]{:S(2)}, u32[]{:S(2)}) %collective-permute-start.6) | collective-permute-done | bytes 524320 | tf_op jit(solution)/shard_map/ppermute | solution.py:114
  195.0 11.3 %collective-permute-done.7 = bf16[512,512]{1,0:T(8,128)(2,1)S(1)} collective-permute-done((bf16[512,512]{1,0:T(8,128)(2,1)S(1)}, bf16[512,512]{1,0:T(8,128)(2,1)S(1)}, u32[]{:S(2)}, u32[]{:S(2)}) %collective-permute-start.7) | collective-permute-done | bytes 524320 | tf_op jit(solution)/shard_map/ppermute | solution.py:114
  207.0 10.7 %collective-permute-done.8 = bf16[512,512]{1,0:T(8,128)(2,1)S(1)} collective-permute-done((bf16[512,512]{1,0:T(8,128)(2,1)S(1)}, bf16[512,512]{1,0:T(8,128)(2,1)S(1)}, u32[]{:S(2)}, u32[]{:S(2)}) %collective-permute-start.8) | collective-permute-done | bytes 524320 | tf_op jit(solution)/shard_map/ppermute | solution.py:114
  217.8 20.8 %all-gather = bf16[16,1,512]{2,1,0:T(2,128)(2,1)S(1)} all-gather(bf16[1,1,512]{2,1,0:T(2,128)(2,1)S(1)} %reshape.106), channel_id=1, replica_groups=mesh['cp'=16,'tp'=2] {'cp'}, dimensions={0}, use_global_device_ids=true | all-gather | bytes 17408 | tf_op jit(solution)/shard_map/all_gather | solution.py:115
  239.7 15.1 %convolution_bitcast_fusion = f32[64,8,16,128]{3,1,2,0:T(8,128)} fusion(bf16[4096,2048]{1,0:T(8,128)(2,1)} %param.15, bf16[512,4096]{1,0:T(8,128)(2,1)} %all-gather.4.cloned.1.call-done, f32[4096]{0:T(1024)S(1)} %copy-done.14, f32[512]{0:T(512)S(1)} %add_rsqrt_fusion), kind=kOutput, calls=%fused_computation.53 | convolution fusion | flops 8598323200 | bytes 25184256 | tf_op jit(solution)/shard_map/dot_general | solution.py:67
  255.0 3.1 copy.86
  260.9 8.9 %collective-permute-done.11 = bf16[512,512]{1,0:T(8,128)(2,1)} collective-permute-done((bf16[512,512]{1,0:T(8,128)(2,1)}, bf16[512,512]{1,0:T(8,128)(2,1)}, u32[]{:S(2)}, u32[]{:S(2)}) %collective-permute-start.11) | collective-permute-done | bytes 524320 | tf_op jit(solution)/shard_map/ppermute | solution.py:114
  271.2 3.0 copy-done
  293.9 2.0 collective-permute-done.13
  305.3 2.1 collective-permute-done.14
  311.7 38.9 %while.24 = (s32[]{:T(128)}, f32[4,4,256]{2,1,0:T(4,128)S(1)}, f32[4,4,256]{2,1,0:T(4,128)S(1)}, f32[4,4,256,128]{3,2,1,0:T(8,128)}, f32[4,4,256]{2,1,0:T(4,128)...) while((s32[]{:T(128)}, f32[4,4,256]{2,1,0:T(4,128)S(1)}, ...), condition=%wide.region_11.12_spmd.clone, body=%wide.region_2.11_spmd.clone.sunk | while | flops 2196522240 | bytes 100160168 | solution.py:162
  313.2 8.1 %conditional.7 = ((f32[4,4,256]{2,1,0:T(4,128)S(1)}, f32[4,4,256]{2,1,0:T(4,128)S(1)}, f32[4,4,256,128]{3,2,1,0:T(8,128)})) conditional(s32[]{:T(128)} %convert_element_type.129, (f32[4,4,256]{2,1,0:T(4,128)S(1)}, f32[4,4,256]{2,1,0:T(4,128)S(1)}, f32[4,4,256,128]{3,2,1,0:T(8,128)}) %tuple.75, (s32[512]{0:T(512)S(1)}, s32[]{:T(128)}, ...), branch_computations={%region_7.7_spmd, %region_8.10_spmd} | conditional | flops 1098260736 | bytes 49029212 | solution.py:157
  315.0 1.7 fusion.24
  316.8 3.2 multiply_add_fusion.2
  321.3 8.0 %conditional.6 = ((f32[4,4,256]{2,1,0:T(4,128)S(1)}, f32[4,4,256]{2,1,0:T(4,128)S(1)}, f32[4,4,256,128]{3,2,1,0:T(8,128)})) conditional(s32[]{:T(128)} %convert_element_type.128, (f32[4,4,256]{2,1,0:T(4,128)S(1)}, f32[4,4,256]{2,1,0:T(4,128)S(1)}, f32[4,4,256,128]{3,2,1,0:T(8,128)}) %tuple.73, (s32[512]{0:T(512)S(1)}, s32[256]{0:T(256)S(1)}, ...), branch_computations={%region_3.3_spmd, %region_4.6_spmd} | conditional | flops 1098260480 | bytes 49027160 | solution.py:154
  324.8 3.2 multiply_add_fusion
  350.6 1.9 copy.69
  352.5 2.9 copy.70
  355.4 2.1 divide_convert_fusion
  357.5 14.1 %convolution_convert_fusion = bf16[512,4096]{1,0:T(8,128)(2,1)} fusion(bf16[2048,4096]{1,0:T(8,128)(2,1)} %param.18, bf16[256,2048]{0,1:T(8,128)(2,1)S(1)} %bitcast.110, bf16[256,2048]{0,1:T(8,128)(2,1)S(1)} %bitcast.111), kind=kOutput, calls=%fused_computation.49 | convolution fusion | flops 8596226048 | bytes 23068672 | tf_op jit(solution)/shard_map/dot_general | solution.py:173
  371.6 294.6 %reduce-scatter.2.cloned.1.call-done = bf16[512,2048]{1,0:T(8,128)(2,1)} async-done(((bf16[512,4096]{1,0:T(8,128)(2,1)}), bf16[512,2048]{1,0:T(8,128)(2,1)}) %reduce-scatter.2.cloned.1.call-update) | async-done | bytes 2097168 | tf_op jit(solution)/shard_map/reduce_scatter | solution.py:174
  (218 shorter events, 72.1 us)
Async XLA Ops:
  6.5 61.8 %all-gather.4.cloned.1.call-start = ((), (), s32[]{:S(2)}) async-start(), calls=%async_computation.1 | async-start | bytes 6291456 | tf_op jit(solution)/shard_map/all_gather | solution.py:61
  7.3 301.3 %all-gather.6.cloned.1.call-start = ((), (), s32[]{:S(2)}) async-start(), calls=%async_computation.2 | async-start | bytes 8912896 | tf_op jit(solution)/shard_map/all_gather | solution.py:103
  15.8 59.6 %copy-start.14 = (f32[4096]{0:T(1024)S(1)}, f32[4096]{0:T(1024)}, u32[]{:S(2)}) copy-start(f32[4096]{0:T(1024)} %param.14) | copy-start | bytes 49156
  75.3 142.4 %copy-start.13 = (s32[512]{0:T(512)S(1)}, s32[512]{0:T(512)}, u32[]{:S(2)}) copy-start(s32[512]{0:T(512)} %param.19) | copy-start | bytes 6148
  75.4 590.8 %reduce-scatter.2.cloned.1.call-start = ((), (), s32[]{:S(2)}) async-start(), calls=%async_computation.3 | async-start | bytes 6291456 | tf_op jit(solution)/shard_map/reduce_scatter | solution.py:174
  81.3 17.1 %collective-permute-start = (bf16[512,512]{1,0:T(8,128)(2,1)S(1)}, bf16[512,512]{1,0:T(8,128)(2,1)S(1)}, u32[]{:S(2)}, u32[]{:S(2)}) collective-permute-start(bf16[512,512]{1,0:T(8,128)(2,1)S(1)} %convolution_convert_fusion.1), channel_id=1, source_target_pairs={{0,2},{2,4},{4,6},{6,8},{8,10},{10,12},{12,14},{14,16},{16,18},{18... | collective-permute-start | bytes 1572872 | tf_op jit(solution)/shard_map/ppermute | solution.py:114
  98.3 108.0 %copy-start.6 = (bf16[512,512]{1,0:T(8,128)(2,1)}, bf16[512,512]{1,0:T(8,128)(2,1)S(1)}, u32[]{:S(2)}) copy-start(bf16[512,512]{1,0:T(8,128)(2,1)S(1)} %collective-permute-done) | copy-start | bytes 1572868
  98.3 17.7 %collective-permute-start.1 = (bf16[512,512]{1,0:T(8,128)(2,1)S(1)}, bf16[512,512]{1,0:T(8,128)(2,1)S(1)}, u32[]{:S(2)}, u32[]{:S(2)}) collective-permute-start(bf16[512,512]{1,0:T(8,128)(2,1)S(1)} %collective-permute-done), channel_id=1, source_target_pairs={{0,2},{2,4},{4,6},{6,8},{8,10},{10,12},{12,14},{14,16},{16,18},{18... | collective-permute-start | bytes 1572872 | tf_op jit(solution)/shard_map/ppermute | solution.py:114
  116.0 90.3 %copy-start.8 = (bf16[512,512]{1,0:T(8,128)(2,1)}, bf16[512,512]{1,0:T(8,128)(2,1)S(1)}, u32[]{:S(2)}) copy-start(bf16[512,512]{1,0:T(8,128)(2,1)S(1)} %collective-permute-done.1) | copy-start | bytes 1572868
  116.0 20.5 %collective-permute-start.2 = (bf16[512,512]{1,0:T(8,128)(2,1)S(1)}, bf16[512,512]{1,0:T(8,128)(2,1)S(1)}, u32[]{:S(2)}, u32[]{:S(2)}) collective-permute-start(bf16[512,512]{1,0:T(8,128)(2,1)S(1)} %collective-permute-done.1), channel_id=1, source_target_pairs={{0,2},{2,4},{4,6},{6,8},{8,10},{10,12},{12,14},{14,16},{16,18},{18... | collective-permute-start | bytes 1572872 | tf_op jit(solution)/shard_map/ppermute | solution.py:114
  136.4 69.8 %copy-start.10 = (bf16[512,512]{1,0:T(8,128)(2,1)}, bf16[512,512]{1,0:T(8,128)(2,1)S(1)}, u32[]{:S(2)}) copy-start(bf16[512,512]{1,0:T(8,128)(2,1)S(1)} %collective-permute-done.2) | copy-start | bytes 1572868
  136.5 22.2 %collective-permute-start.3 = (bf16[512,512]{1,0:T(8,128)(2,1)S(1)}, bf16[512,512]{1,0:T(8,128)(2,1)S(1)}, u32[]{:S(2)}, u32[]{:S(2)}) collective-permute-start(bf16[512,512]{1,0:T(8,128)(2,1)S(1)} %collective-permute-done.2), channel_id=1, source_target_pairs={{0,2},{2,4},{4,6},{6,8},{8,10},{10,12},{12,14},{14,16},{16,18},{18... | collective-permute-start | bytes 1572872 | tf_op jit(solution)/shard_map/ppermute | solution.py:114
  158.6 47.7 %copy-start.11 = (bf16[512,512]{1,0:T(8,128)(2,1)}, bf16[512,512]{1,0:T(8,128)(2,1)S(1)}, u32[]{:S(2)}) copy-start(bf16[512,512]{1,0:T(8,128)(2,1)S(1)} %collective-permute-done.3) | copy-start | bytes 1572868
  158.6 13.7 %collective-permute-start.4 = (bf16[512,512]{1,0:T(8,128)(2,1)S(1)}, bf16[512,512]{1,0:T(8,128)(2,1)S(1)}, u32[]{:S(2)}, u32[]{:S(2)}) collective-permute-start(bf16[512,512]{1,0:T(8,128)(2,1)S(1)} %collective-permute-done.3), channel_id=1, source_target_pairs={{0,2},{2,4},{4,6},{6,8},{8,10},{10,12},{12,14},{14,16},{16,18},{18... | collective-permute-start | bytes 1572872 | tf_op jit(solution)/shard_map/ppermute | solution.py:114
  172.4 11.3 %collective-permute-start.5 = (bf16[512,512]{1,0:T(8,128)(2,1)S(1)}, bf16[512,512]{1,0:T(8,128)(2,1)S(1)}, u32[]{:S(2)}, u32[]{:S(2)}) collective-permute-start(bf16[512,512]{1,0:T(8,128)(2,1)S(1)} %collective-permute-done.4), channel_id=1, source_target_pairs={{0,2},{2,4},{4,6},{6,8},{8,10},{10,12},{12,14},{14,16},{16,18},{18... | collective-permute-start | bytes 1572872 | tf_op jit(solution)/shard_map/ppermute | solution.py:114
  183.7 11.3 %collective-permute-start.6 = (bf16[512,512]{1,0:T(8,128)(2,1)S(1)}, bf16[512,512]{1,0:T(8,128)(2,1)S(1)}, u32[]{:S(2)}, u32[]{:S(2)}) collective-permute-start(bf16[512,512]{1,0:T(8,128)(2,1)S(1)} %collective-permute-done.5), channel_id=1, source_target_pairs={{0,2},{2,4},{4,6},{6,8},{8,10},{10,12},{12,14},{14,16},{16,18},{18... | collective-permute-start | bytes 1572872 | tf_op jit(solution)/shard_map/ppermute | solution.py:114
  195.0 11.7 %copy-start.5 = (bf16[512,512]{1,0:T(8,128)(2,1)}, bf16[512,512]{1,0:T(8,128)(2,1)S(1)}, u32[]{:S(2)}) copy-start(bf16[512,512]{1,0:T(8,128)(2,1)S(1)} %collective-permute-done.6) | copy-start | bytes 1572868
  195.0 11.3 %collective-permute-start.7 = (bf16[512,512]{1,0:T(8,128)(2,1)S(1)}, bf16[512,512]{1,0:T(8,128)(2,1)S(1)}, u32[]{:S(2)}, u32[]{:S(2)}) collective-permute-start(bf16[512,512]{1,0:T(8,128)(2,1)S(1)} %collective-permute-done.6), channel_id=1, source_target_pairs={{0,2},{2,4},{4,6},{6,8},{8,10},{10,12},{12,14},{14,16},{16,18},{18... | collective-permute-start | bytes 1572872 | tf_op jit(solution)/shard_map/ppermute | solution.py:114
  206.3 48.5 %copy-start.7 = (bf16[512,512]{1,0:T(8,128)(2,1)}, bf16[512,512]{1,0:T(8,128)(2,1)S(1)}, u32[]{:S(2)}) copy-start(bf16[512,512]{1,0:T(8,128)(2,1)S(1)} %collective-permute-done.7) | copy-start | bytes 1572868
  206.3 11.4 %collective-permute-start.8 = (bf16[512,512]{1,0:T(8,128)(2,1)S(1)}, bf16[512,512]{1,0:T(8,128)(2,1)S(1)}, u32[]{:S(2)}, u32[]{:S(2)}) collective-permute-start(bf16[512,512]{1,0:T(8,128)(2,1)S(1)} %collective-permute-done.7), channel_id=1, source_target_pairs={{0,2},{2,4},{4,6},{6,8},{8,10},{10,12},{12,14},{14,16},{16,18},{18... | collective-permute-start | bytes 1572872 | tf_op jit(solution)/shard_map/ppermute | solution.py:114
  217.7 37.1 %copy-start.9 = (bf16[512,512]{1,0:T(8,128)(2,1)}, bf16[512,512]{1,0:T(8,128)(2,1)S(1)}, u32[]{:S(2)}) copy-start(bf16[512,512]{1,0:T(8,128)(2,1)S(1)} %collective-permute-done.8) | copy-start | bytes 1572868
  217.7 21.1 %collective-permute-start.9 = (bf16[512,512]{1,0:T(8,128)(2,1)S(1)}, bf16[512,512]{1,0:T(8,128)(2,1)}, u32[]{:S(2)}, u32[]{:S(2)}) collective-permute-start(bf16[512,512]{1,0:T(8,128)(2,1)S(1)} %collective-permute-done.8), channel_id=1, source_target_pairs={{0,2},{2,4},{4,6},{6,8},{8,10},{10,12},{12,14},{14,16},{16,18},{18... | collective-permute-start | bytes 1572872 | tf_op jit(solution)/shard_map/ppermute | solution.py:114
  238.8 19.3 %collective-permute-start.10 = (bf16[512,512]{1,0:T(8,128)(2,1)}, bf16[512,512]{1,0:T(8,128)(2,1)}, u32[]{:S(2)}, u32[]{:S(2)}) collective-permute-start(bf16[512,512]{1,0:T(8,128)(2,1)} %collective-permute-done.9), channel_id=1, source_target_pairs={{0,2},{2,4},{4,6},{6,8},{8,10},{10,12},{12,14},{14,16},{16,18},{18... | collective-permute-start | bytes 1572872 | tf_op jit(solution)/shard_map/ppermute | solution.py:114
  258.1 11.7 %collective-permute-start.11 = (bf16[512,512]{1,0:T(8,128)(2,1)}, bf16[512,512]{1,0:T(8,128)(2,1)}, u32[]{:S(2)}, u32[]{:S(2)}) collective-permute-start(bf16[512,512]{1,0:T(8,128)(2,1)} %collective-permute-done.10), channel_id=1, source_target_pairs={{0,2},{2,4},{4,6},{6,8},{8,10},{10,12},{12,14},{14,16},{16,18},{18... | collective-permute-start | bytes 1572872 | tf_op jit(solution)/shard_map/ppermute | solution.py:114
  269.8 14.4 %collective-permute-start.12 = (bf16[512,512]{1,0:T(8,128)(2,1)}, bf16[512,512]{1,0:T(8,128)(2,1)}, u32[]{:S(2)}, u32[]{:S(2)}) collective-permute-start(bf16[512,512]{1,0:T(8,128)(2,1)} %collective-permute-done.11), channel_id=1, source_target_pairs={{0,2},{2,4},{4,6},{6,8},{8,10},{10,12},{12,14},{14,16},{16,18},{18... | collective-permute-start | bytes 1572872 | tf_op jit(solution)/shard_map/ppermute | solution.py:114
  270.9 3.3 copy-start
  284.2 11.7 %collective-permute-start.13 = (bf16[512,512]{1,0:T(8,128)(2,1)}, bf16[512,512]{1,0:T(8,128)(2,1)}, u32[]{:S(2)}, u32[]{:S(2)}) collective-permute-start(bf16[512,512]{1,0:T(8,128)(2,1)} %collective-permute-done.12), channel_id=1, source_target_pairs={{0,2},{2,4},{4,6},{6,8},{8,10},{10,12},{12,14},{14,16},{16,18},{18... | collective-permute-start | bytes 1572872 | tf_op jit(solution)/shard_map/ppermute | solution.py:114
  295.9 11.5 %collective-permute-start.14 = (bf16[512,512]{1,0:T(8,128)(2,1)}, bf16[512,512]{1,0:T(8,128)(2,1)S(1)}, u32[]{:S(2)}, u32[]{:S(2)}) collective-permute-start(bf16[512,512]{1,0:T(8,128)(2,1)} %collective-permute-done.13), channel_id=1, source_target_pairs={{0,2},{2,4},{4,6},{6,8},{8,10},{10,12},{12,14},{14,16},{16,18},{18... | collective-permute-start | bytes 1572872 | tf_op jit(solution)/shard_map/ppermute | solution.py:114
  313.4 3.3 copy-start.3
  319.9 1.3 copy-start.4
  321.5 3.3 copy-start.1
  328.0 1.3 copy-start.2
  (1 other events, 0.8 us)
Sparse Core Ops, SparseCore 0:
  8.9 59.4 all-gather.3
  75.5 90.2 all-gather.5
  371.7 294.4 reduce-scatter.1
